TPU v7x, 32 devices: a whole 2x2x4 slice. The times are simulated.
32 devices in a mesh: band: 2 (over x), tm: 16 (over z, y, core).
Axes of the slice: x: 2, y: 2, z: 4, core: 2. Of those that a mesh axis runs over, the one named last changes fastest.
Arguments:
- voltages: bfloat16 [16, 2, 512, 4096], P('band', None, None, 'tm'), parts along dimension 0, may hold values from -12 to 12
- antenna_flags: int32 [32, 16], P('tm', 'band'), parts along dimension 1, may hold values from -2147483648 to 2147483647, as said below
- owned_tile: int32 [16], replicated, may hold values from 0 to 15, each once
Outputs:
- visibility: float32 [512, 16, 2, 512], P('tm', 'band'), parts along dimension 1
There are 2 independent parts, one for each index of `band`. A program takes and returns all parts, laid end to end along the dimension named above; an argument that names none is the same for every part. Nothing has to cross between parts.
Inputs may be any that keep to these rules, and one draw needn't show every extreme that they name: `antenna_flags`: bit b of word w of sub-integration s is 1 where the samples of both polarisations of antenna 32 * w + b are good in that sub-integration of 128 samples, 0 where flagged; all 32 bits of a word are used; some antennas may be flagged in every sub-integration. A permutation: the index k of tm holds the baseline rows of tile owned_tile[k].
All inputs are finite; a program needn't handle non-finite values.
Results may differ from a plain program's by a relative error of at most 0.0003.
Values sent between devices are 32-bit elements; how exact they have to be, the bound alone decides.
No kernel may reach another device: no remote copies, remote signals or barrier semaphores. Data moves between devices by JAX's collectives and lax.ppermute only.
A program may use at most 128 MiB of HBM per device.

v0:
```python
import jax
import jax.numpy as jnp
from jax import lax
from jax.sharding import PartitionSpec as P


def unpack_flags(words):
    shifts = jnp.arange(32, dtype=jnp.int32)
    bits = jnp.bitwise_and(jnp.right_shift(words[:, :, None], shifts[None, None, :]), 1)
    return bits.reshape(words.shape[0], words.shape[1] * 32)


def stack_operands(masked):
    real_part = masked[:, 0]
    imag_part = masked[:, 1]
    right_side = jnp.concatenate([real_part, imag_part], axis=-1)
    left_side = jnp.stack([right_side, jnp.concatenate([imag_part, -real_part], axis=-1)], axis=1)
    return (left_side, right_side)


def shards(voltages, antenna_flags, owned_tile):
    axis_count = lax.axis_size("tm")
    my_index = lax.axis_index("tm")
    inputs = voltages.shape[2]
    samples = voltages.shape[3]
    block_rows = inputs // axis_count
    sub_length = samples // antenna_flags.shape[0]
    every_word = lax.all_gather(antenna_flags, "tm", axis=0, tiled=True)
    every_flag = unpack_flags(every_word)
    local_flag = unpack_flags(antenna_flags)
    own_tile = owned_tile[my_index]
    own_antennas = (own_tile * block_rows + jnp.arange(block_rows, dtype=jnp.int32)) // 2
    own_flags = jnp.take(every_flag, own_antennas, axis=1)
    input_flags = jnp.repeat(every_flag, 2, axis=1)
    counts = sub_length * jnp.dot(own_flags.T, input_flags)
    divisor = jnp.maximum(counts, 1).astype(jnp.float32)[:, None, None, :]
    sample_flags = jnp.repeat(jnp.repeat(local_flag, 2, axis=1).T, sub_length, axis=1).astype(
        jnp.bfloat16
    )
    masked = voltages * sample_flags[None, None]
    left_side, right_side = stack_operands(masked)
    row_index = (
        owned_tile[:, None] * block_rows + jnp.arange(block_rows, dtype=jnp.int32)[None, :]
    ).reshape(-1)
    picked = jnp.take(left_side, row_index, axis=2)
    summed = lax.psum_scatter(
        jnp.einsum("ckru,cju->rckj", picked, right_side, preferred_element_type=jnp.float32),
        "tm",
        scatter_dimension=0,
        tiled=True,
    )
    return summed / divisor


def solution(mesh):
    return jax.shard_map(
        shards,
        mesh=mesh,
        in_specs=(P("band", None, None, "tm"), P("tm", "band"), P()),
        out_specs=P("tm", "band", None, None),
        check_vma=False,
    )
```

profile of v0, /device:TPU:0, one launch (start us, length us, event | category | flops | bytes accessed | tf_op | source)
XLA Modules:
  0.0 301.0 jit_solution(14204660816384712198)
XLA Ops:
  6.5 0.1 shift_right_arithmetic.43
  6.6 0.8 copy.18
  7.4 0.1 fusion.7
  7.6 0.6 broadcast_in_dim.38
  8.2 2.7 copy_multiply_fusion
  10.9 1.7 slice_bitcast_fusion.1
  12.5 1.5 fusion.14
  14.1 0.1 add.111
  14.2 6.3 %fusion.2 = (bf16[8,1,512,512]{3,2,0,1:T(8,128)(2,1)}, bf16[8,1,512,512]{3,2,0,1:T(8,128)(2,1)}) fusion(bf16[8,512,256]{2,1,0:T(8,128)(2,1)} %get-tuple-element.6, bf16[8,512,256]{2,1,0:T(8,128)(2,1)S(1)} %get-tuple-element.5, bf16[8,512,256]{2,1,0:T(8,128)(2,1)} %fusion.14), kind=kLoop, calls=%fused_computation.10 | loop fusion | flops 16777216 | bytes 14680064 | tf_op jit(solution)/shard_map/stack | solution.py:17
  20.6 7.4 %pad_maximum_fusion = bf16[8,2,512,512]{3,2,0,1:T(8,128)(2,1)} fusion(bf16[8,1,512,512]{3,2,0,1:T(8,128)(2,1)} %get-tuple-element.8, bf16[8,1,512,512]{3,2,0,1:T(8,128)(2,1)} %get-tuple-element.7), kind=kLoop, calls=%fused_computation.3 | loop fusion | flops 4194304 | bytes 16777216 | tf_op jit(solution)/shard_map/stack | solution.py:17
  28.0 11.3 %copy.20 = bf16[8,2,512,512]{3,0,2,1:T(8,128)(2,1)} copy(bf16[8,2,512,512]{3,2,0,1:T(8,128)(2,1)} %pad_maximum_fusion) | data formatting | bytes 16777216 | tf_op jit(solution)/shard_map/stack | solution.py:17
  39.4 23.2 %gather_fusion = bf16[512,8,2,512]{3,1,2,0:T(8,128)(2,1)} fusion(bf16[8,2,512,512]{3,0,2,1:T(8,128)(2,1)} %copy.20, s32[1024]{0:T(1024)S(1)} %pad_clamp_fusion.1), kind=kCustom, calls=%fused_computation | custom fusion | bytes 16779264 | tf_op jit(solution)/shard_map/jit(_take)/gather | solution.py:45
  62.6 7.6 %select_bitcast_fusion = bf16[8,2,512,512]{3,0,1,2:T(8,128)(2,1)} fusion(bf16[512,8,2,512]{3,1,2,0:T(8,128)(2,1)} %gather_fusion, pred[512]{0:T(512)(128)(4,1)S(1)} %compare_and_fusion.1), kind=kLoop, calls=%fused_computation.5 | loop fusion | flops 4194304 | bytes 16777728 | tf_op jit(solution)/shard_map/jit(_take)/select_n | solution.py:45
  70.2 20.3 %convolution_bitcast_fusion = f32[512,8,2,512]{0,3,2,1:T(8,128)} fusion(bf16[8,2,512,512]{3,0,1,2:T(8,128)(2,1)} %select_bitcast_fusion, bf16[8,512,256]{2,1,0:T(8,128)(2,1)} %get-tuple-element.6, bf16[8,512,256]{2,1,0:T(8,128)(2,1)S(1)} %get-tuple-element.5), kind=kOutput, calls=%fused_computation.2 | convolution fusion | flops 4303355904 | bytes 29360128 | tf_op jit(solution)/shard_map/ckru,cju->rckj/dot_general | solution.py:47
  90.6 20.2 %copy.22 = f32[512,8,2,512]{3,1,2,0:T(8,128)} copy(f32[512,8,2,512]{0,3,2,1:T(8,128)} %convolution_bitcast_fusion) | data formatting | bytes 33554432 | tf_op jit(solution)/shard_map/ckru,cju->rckj/transpose | solution.py:47
  110.8 0.6 dynamic_slice.3
  111.5 23.1 %all-gather = s32[16,2,8]{2,1,0:T(2,128)S(1)} all-gather(s32[1,2,8]{2,1,0:T(2,128)S(1)} %bitcast.50), channel_id=1, replica_groups=mesh['band'=2,'tm'=16] {'tm'}, dimensions={0}, use_global_device_ids=true | all-gather | bytes 1088 | tf_op jit(solution)/shard_map/all_gather | solution.py:28
  134.7 0.1 fusion.5
  135.5 0.6 gather_fusion.1
  136.1 0.1 broadcast_in_dim.43
  136.2 0.6 fusion.4
  136.8 154.3 %reduce-scatter.2.cloned.1.call-done = f32[32,8,2,512]{3,1,2,0:T(8,128)} async-done(((f32[512,8,2,512]{3,1,2,0:T(8,128)}), f32[32,8,2,512]{3,1,2,0:T(8,128)}) %reduce-scatter.2.cloned.1.call-update) | async-done | bytes 1048592 | tf_op jit(solution)/shard_map/reduce_scatter | solution.py:46
  291.0 1.4 broadcast_divide_fusion
  292.4 1.8 copy.24
  (19 shorter events, 0.5 us)
Async XLA Ops:
  6.5 284.5 %reduce-scatter.2.cloned.1.call-start = ((), (), s32[]{:S(2)}) async-start(), calls=%async_computation.1 | async-start | bytes 17825792 | tf_op jit(solution)/shard_map/reduce_scatter | solution.py:46
  10.9 3.1 %copy-start.1 = (s32[16]{0:T(128)S(1)}, s32[16]{0:T(128)}, u32[]{:S(2)}) copy-start(s32[16]{0:T(128)} %param.5) | copy-start | bytes 196
  110.8 0.7 copy-start
Sparse Core Ops, SparseCore 0:
  110.9 180.0 reduce-scatter.1
where the time goes:
time: 302 us; the launch traced here: 301 us
  waiting for transfers between devices  154 us (51%)
  local copies, waits for them, and re-layouts  61.3 us (20%)
  other arithmetic  27.2 us (9%)
  blocking collectives  23.1 us (8%)
  matrix products  20.9 us (7%)
  between operations  14.2 us (5%)
    reduce_scatter x1, waiting for transfers between devices, shards(): lax.psum_scatter(jnp.einsum('ckru,cju->rckj', picked, right_side, preferr...  154 us
    gather x1, local copies, waits for them, and re-layouts, shards(): picked = jnp.take(left_side, row_index, axis=2)  23.2 us
    all_gather x1, blocking collectives, shards(): every_word = lax.all_gather(antenna_flags, 'tm', axis=0, tiled=True)  23.1 us
    dot_general x1, matrix products, shards(): jnp.einsum('ckru,cju->rckj', picked, right_side, preferred_element_type=j...  20.3 us
    transpose x1, local copies, waits for them, and re-layouts, shards(): jnp.einsum('ckru,cju->rckj', picked, right_side, preferred_element_type=j...  20.2 us
    another operation x2, other arithmetic, stack_operands(): jnp.stack([right_side, jnp.concatenate([imag_part, -real_part], axis=-1)]...  13.8 us
    another operation x1, local copies, waits for them, and re-layouts, stack_operands(): jnp.stack([right_side, jnp.concatenate([imag_part, -real_part], axis=-1)]...  11.3 us
    select_n x2, other arithmetic, shards(): picked = jnp.take(left_side, row_index, axis=2)  7.63 us
  transfers between devices with their start and end apart: 1, of which 1 were waited for; matrix products, arithmetic and copies ran while one was open for 1% of the time, Pallas kernels for 0%

commit v1 on v0

--- a/solution.py
+++ b/solution.py
@@ -1,7 +1,12 @@
 import jax
 import jax.numpy as jnp
 from jax import lax
+from jax.experimental import pallas as pl
+from jax.experimental.pallas import tpu as pltpu
 from jax.sharding import PartitionSpec as P
+
+
+LANES = 128
 
 
 def unpack_flags(words):
@@ -18,7 +23,7 @@
     return (left_side, right_side)
 
 
-def shards(voltages, antenna_flags, owned_tile):
+def plain_shards(voltages, antenna_flags, owned_tile):
     axis_count = lax.axis_size("tm")
     my_index = lax.axis_index("tm")
     inputs = voltages.shape[2]
@@ -52,7 +57,440 @@
     return summed / divisor
 
 
+def line_of_chips(mesh):
+    columns = mesh.devices.reshape(-1, mesh.shape["tm"])
+    count = columns.shape[1]
+    if count % 4:
+        return None
+    for column in columns:
+        places = []
+        for device in column:
+            coords = getattr(device, "coords", None)
+            core = getattr(device, "core_on_chip", None)
+            if coords is None or core is None:
+                return None
+            places.append((coords[2], coords[1], coords[0], core))
+        zs = sorted({p[0] for p in places})
+        ys = sorted({p[1] for p in places})
+        if len(ys) != 2 or len({p[2] for p in places}) != 1 or len(zs) * 4 != count:
+            return None
+        want = [(z, y, places[0][2], core) for z in zs for y in ys for core in (0, 1)]
+        if places != want:
+            return None
+    return count // 4
+
+
+def fill_mask(mask_ref, tile_ref, flag_ref, slots, rows, subs, sub_length):
+    antennas = rows // 2
+    row = lax.broadcasted_iota(jnp.int32, (rows, sub_length), 0)
+    for k in range(slots):
+        first = tile_ref[k] * antennas
+        shift = first % 32 + row // 2
+        for s in range(subs):
+            word = flag_ref[s, first // 32]
+            bit = lax.shift_right_arithmetic(jnp.full((rows, sub_length), word, jnp.int32), shift) & 1
+            mask_ref[k * rows : (k + 1) * rows, s * sub_length : (s + 1) * sub_length] = bit.astype(
+                jnp.float32
+            ).astype(jnp.bfloat16)
+
+
+def gram_step(c, x_ref, T, y, core, store, load, p_ref, *, groups, rows, channels):
+    quarter = LANES // rows
+    span = groups // 2 + 1
+
+    def both(g):
+        at = pl.ds(pl.multiple_of(g * LANES, LANES), LANES)
+        return x_ref[c, 0, at, :], x_ref[c, 1, at, :]
+
+    real, imag = both(T)
+    left = jnp.concatenate(
+        [jnp.concatenate([real, imag], axis=1), jnp.concatenate([imag, -real], axis=1)], axis=0
+    )
+    right = jnp.concatenate(
+        [jnp.concatenate(both((T + g) % groups), axis=1) for g in range(span)], axis=0
+    )
+    p_ref[...] = lax.dot_general(
+        left, right, (((1,), (1,)), ((), ())), preferred_element_type=jnp.float32
+    )
+    lane = lax.broadcasted_iota(jnp.int32, (rows, LANES), 1)
+    edge = slice((span - 1) * LANES, span * LANES)
+    j = c % quarter
+    tail = channels * 2 * (span - 1) + c // quarter
+    for dest, parity in ((0, core), (1, 1 - core)):
+        for slot_y in range(2):
+            r = 2 * (y if slot_y == 0 else 1 - y) + parity
+            shift = r * rows
+            for ri in range(2):
+                at = pl.ds(pl.multiple_of(ri * LANES + shift, rows), rows)
+                last = p_ref[at, edge]
+                for g in range(span - 1):
+                    block = p_ref[at, g * LANES : (g + 1) * LANES]
+                    if g == 0:
+                        block = jnp.where(lane < shift, last, block)
+                    store(dest, slot_y, (c * 2 + ri) * (span - 1) + g, block)
+            across = jnp.where(T < groups // 2, 0, LANES)
+            last = p_ref[pl.ds(pl.multiple_of(across + shift, rows), rows), edge]
+            moved = pltpu.roll(last, (rows * (j - r + quarter)) % LANES, axis=1)
+            old = load(dest, slot_y, tail)
+            store(dest, slot_y, tail, jnp.where(lane // rows == j, moved, old))
+
+
+def my_place(places):
+    me = lax.axis_index("tm")
+    z = me // 4
+    order = []
+    for i in range(places):
+        target = jnp.int32(ORDER[0][i])
+        for other in range(1, places):
+            target = jnp.where(z == other, ORDER[other][i], target)
+        order.append(target)
+    return order + [(me // 2) % 2, me % 2, me]
+
+
+def first_kernel(
+    tile_ref, flag_ref, v_ref, x_ref, own_ref, send_ref, word_ref, raw_ref, mask_ref, p_ref, sems, *, slots, subs, **kw
+):
+    channels, rows = kw["channels"], kw["rows"]
+
+    def fetch(c):
+        return pltpu.make_async_copy(v_ref.at[c], raw_ref.at[c], sems.at[c])
+
+    for c in range(channels):
+        fetch(c).start()
+    fill_mask(mask_ref, tile_ref, flag_ref, slots, rows, subs, v_ref.shape[3] // subs)
+    spread = word_ref.shape
+    here = lax.broadcasted_iota(jnp.int32, spread, 0) - lax.axis_index("tm") * subs
+    column = lax.broadcasted_iota(jnp.int32, spread, 1)
+    words = jnp.zeros(spread, jnp.int32)
+    for sub in range(subs):
+        for w in range(spread[1]):
+            words = jnp.where((here == sub) & (column == w), flag_ref[sub, w], words)
+    word_ref[...] = words
+    places = len(ORDER)
+    place_ref = my_place(places)
+    refs = (own_ref, send_ref)
+
+    def store(dest, slot_y, block, value):
+        refs[dest][slot_y, block] = value
+
+    def load(dest, slot_y, block):
+        return refs[dest][slot_y, block]
+
+    def body(c, carry):
+        fetch(c).wait()
+        for k in range(slots):
+            at = pl.ds(pl.multiple_of(tile_ref[k] * rows, rows), rows)
+            for ri in range(2):
+                x_ref[c, ri, k * rows : (k + 1) * rows, :] = (
+                    raw_ref[c, ri, at, :] * mask_ref[k * rows : (k + 1) * rows, :]
+                )
+        gram_step(c, x_ref, place_ref[0], place_ref[places], place_ref[places + 1], store, load, p_ref, **kw)
+        return carry
+
+    lax.fori_loop(0, channels, body, 0)
+
+
+def next_kernel(x_ref, own_ref, send_ref, p_ref, *, part, **kw):
+    places = len(ORDER)
+    place_ref = my_place(places)
+    refs = (own_ref, send_ref)
+
+    def store(dest, slot_y, block, value):
+        refs[dest][slot_y, block] = value
+
+    def load(dest, slot_y, block):
+        return refs[dest][slot_y, block]
+
+    def body(c, carry):
+        gram_step(c, x_ref, place_ref[part], place_ref[places], place_ref[places + 1], store, load, p_ref, **kw)
+        return carry
+
+    lax.fori_loop(0, kw["channels"], body, 0)
+
+
+def join_kernel(own_ref, got_ref, away_ref, kept_ref):
+    away_ref[...] = own_ref[1] + got_ref[1]
+    kept_ref[...] = own_ref[0] + got_ref[0]
+
+
+def sum_kernel(*refs):
+    total = refs[0][...] + refs[1][...]
+    for ref in refs[2:-1]:
+        total = total + ref[...]
+    refs[-1][...] = total
+
+
+def mirror_kernel(a_ref, b_ref, c_ref, d_ref, e_ref, z_ref, *refs, channels, rows, slots, span):
+    messages, tr_ref = refs[:-1], refs[-1]
+    places = len(ORDER)
+    place_ref = my_place(places)
+    r = place_ref[places] * 2 + place_ref[places + 1]
+    quarter = LANES // rows
+    cells = (span - 1) * quarter
+    z_ref[...] = (a_ref[...] + b_ref[...]) + ((c_ref[...] + d_ref[...]) + e_ref[...])
+    packs = channels // quarter
+    for ri in range(2):
+        for g in range(span - 1):
+            for h in range(packs):
+                block = jnp.concatenate(
+                    [z_ref[((h * quarter + j) * 2 + ri) * (span - 1) + g] for j in range(quarter)], axis=0
+                )
+                turned = block.T
+                tr_ref[g, ri * packs + h] = -turned if ri else turned
+    for delta in range(1, cells):
+        q = (r + delta) % cells
+        at = pl.ds(pl.multiple_of((q % quarter) * rows, rows), rows)
+        for i in range(2 * packs):
+            messages[delta - 1][i] = tr_ref[q // quarter, i, at, :]
+    lane = lax.broadcasted_iota(jnp.int32, (rows, LANES), 1)
+    main = channels * 2 * (span - 1)
+    low = place_ref[places + 2] < slots // 2
+    for h in range(packs):
+        turned = jnp.concatenate([z_ref[main + h]] * quarter, axis=0).T
+        piece = turned[0:rows]
+        for j in range(1, quarter):
+            piece = jnp.where(lane // rows == j, turned[j * rows : (j + 1) * rows], piece)
+        messages[cells - 1][h] = jnp.where(low, piece, -piece)
+
+
+def scale_kernel(tile_ref, word_ref, out_ref, count_ref, *, rows, sub_length):
+    inputs = out_ref.shape[1]
+    words = word_ref[...]
+    subs = words.shape[0]
+    lane = lax.broadcasted_iota(jnp.int32, (subs, LANES), 1)
+    parts = []
+    for g in range(inputs // LANES):
+        low, high = words[:, 2 * g : 2 * g + 1], words[:, 2 * g + 1 : 2 * g + 2]
+        word = jnp.where(lane < LANES // 2, low, high)
+        parts.append(lax.shift_right_arithmetic(word, (lane % (LANES // 2)) // 2) & 1)
+    good = jnp.concatenate(parts, axis=1).astype(jnp.float32).astype(jnp.bfloat16)
+    count_ref[...] = lax.dot_general(
+        good, good, (((0,), (0,)), ((), ())), preferred_element_type=jnp.float32
+    )
+    me = lax.axis_index("tm")
+    first = pl.multiple_of(tile_ref[me] * rows, rows)
+    counts = count_ref[pl.ds(first, rows), :] * float(sub_length)
+    out_ref[...] = 1.0 / jnp.maximum(counts, 1.0)
+
+
+def final_kernel(tile_ref, z_ref, scale_ref, *refs, channels, rows, slots, span):
+    quarter = LANES // rows
+    cells = (span - 1) * quarter
+    packs = channels // quarter
+    main = channels * 2 * (span - 1)
+    messages, out_ref, all_ref, slot_ref = refs[:cells], refs[cells], refs[cells + 1], refs[cells + 2]
+    places = len(ORDER)
+    place_ref = my_place(places)
+    me = place_ref[places + 2]
+    r = place_ref[places] * 2 + place_ref[places + 1]
+    lane = lax.broadcasted_iota(jnp.int32, (rows, LANES), 1) // rows
+    low = jnp.where(me < slots // 2, 1, 0)
+    first = main + packs
+    all_ref[0:first] = z_ref[...]
+    for delta in range(1, cells):
+        at = first + (delta - 1) * 2 * packs
+        all_ref[at : at + 2 * packs] = messages[delta - 1][...]
+    last = first + (cells - 1) * 2 * packs
+    all_ref[last : last + packs] = messages[cells - 1][...]
+    for k in range(slots):
+        slot_ref[tile_ref[k]] = k
+
+    def body(c, carry):
+        j = c % quarter
+        h = c // quarter
+        for group in range(slots // quarter):
+            pieces = [[], []]
+            for there in range(quarter):
+                delta = (slot_ref[group * quarter + there] - me + slots) % slots
+                q = (r + delta) % cells
+                ahead = delta < cells
+                behind = delta > cells
+                here = jnp.where(ahead, q % quarter, j)
+                shift = (rows * (there - here + quarter)) % LANES
+                for ri in range(2):
+                    mine = low if ri == 0 else 1 - low
+                    at = jnp.where(
+                        ahead,
+                        (c * 2 + ri) * (span - 1) + q // quarter,
+                        jnp.where(
+                            behind,
+                            first + (slots - 1 - delta) * 2 * packs + ri * packs + h,
+                            jnp.where(mine == 1, main, last) + h,
+                        ),
+                    )
+                    pieces[ri].append(pltpu.roll(all_ref[at], shift, axis=1))
+            scale = scale_ref[:, group * LANES : (group + 1) * LANES]
+            for ri in range(2):
+                value = pieces[ri][0]
+                for there in range(1, quarter):
+                    value = jnp.where(lane == there, pieces[ri][there], value)
+                out_ref[:, c, ri, group * LANES : (group + 1) * LANES] = value * scale
+        return carry
+
+    for c in range(channels):
+        body(c, 0)
+
+
+ORDER = ((3, 2, 1, 0), (0, 3, 2, 1), (3, 0, 1, 2), (0, 1, 2, 3))
+HOPS = (2, 1, 4, 8)
+
+
+def inverse_counts(words, owned_tile, slots, rows, inputs, sub_length):
+    smem = pl.BlockSpec(memory_space=pltpu.SMEM)
+    vmem = pl.BlockSpec(memory_space=pltpu.VMEM)
+    for hop in HOPS:
+        words = words + lax.ppermute(words, "tm", [(d, d ^ hop) for d in range(slots)])
+    return pl.pallas_call(
+        lambda *refs: scale_kernel(*refs, rows=rows, sub_length=sub_length),
+        in_specs=[smem, vmem],
+        out_specs=vmem,
+        out_shape=jax.ShapeDtypeStruct((rows, inputs), jnp.float32),
+        scratch_shapes=[pltpu.VMEM((inputs, inputs), jnp.float32)],
+        compiler_params=pltpu.CompilerParams(vmem_limit_bytes=4 << 20),
+        name="scale",
+    )(owned_tile, words)
+
+
+def grid_shards(voltages, antenna_flags, owned_tile, places):
+    slots = lax.axis_size("tm")
+    channels, _, inputs, samples = voltages.shape
+    rows = inputs // slots
+    subs = antenna_flags.shape[0]
+    groups = inputs // LANES
+    span = groups // 2 + 1
+    quarter = LANES // rows
+    packs = channels // quarter
+    blocks = channels * 2 * (span - 1) + packs
+    smem = pl.BlockSpec(memory_space=pltpu.SMEM)
+    vmem = pl.BlockSpec(memory_space=pltpu.VMEM)
+    size = dict(groups=groups, rows=rows, channels=channels)
+    product = pltpu.VMEM((2 * LANES, span * LANES), jnp.float32)
+
+    work = 4 * channels * LANES * inputs * samples * 8
+
+    def chunk(*lead):
+        return jax.ShapeDtypeStruct(lead + (blocks, rows, LANES), jnp.float32)
+
+    def limit(mib):
+        return pltpu.CompilerParams(vmem_limit_bytes=mib << 20)
+
+    masked, own, send, words = pl.pallas_call(
+        lambda *refs: first_kernel(*refs, slots=slots, subs=subs, **size),
+        in_specs=[smem, smem, pl.BlockSpec(memory_space=pltpu.HBM)],
+        out_specs=[vmem] * 4,
+        out_shape=[jax.ShapeDtypeStruct(voltages.shape, jnp.bfloat16), chunk(2), chunk(2), jax.ShapeDtypeStruct((slots * subs, antenna_flags.shape[1]), jnp.int32)],
+        scratch_shapes=[
+            pltpu.VMEM(voltages.shape, jnp.bfloat16),
+            pltpu.VMEM((inputs, samples), jnp.bfloat16),
+            product,
+            pltpu.SemaphoreType.DMA((channels,)),
+        ],
+        compiler_params=limit(16),
+        cost_estimate=pl.CostEstimate(flops=work, bytes_accessed=0, transcendentals=0),
+        name="mask_and_part",
+    )(owned_tile, antenna_flags, pltpu.with_memory_space_constraint(voltages, pltpu.HBM))
+    parts = [(own, send)]
+    for i in range(1, places):
+        parts.append(
+            pl.pallas_call(
+                lambda *refs: next_kernel(*refs, part=i, **size),
+                in_specs=[vmem],
+                out_specs=[vmem] * 2,
+                out_shape=[chunk(2)] * 2,
+                scratch_shapes=[product],
+                compiler_params=limit(16),
+                cost_estimate=pl.CostEstimate(flops=work, bytes_accessed=0, transcendentals=0),
+            )(masked)
+        )
+
+    other_core = [(d, d ^ 1) for d in range(slots)]
+    other_y = [(d, d ^ 2) for d in range(slots)]
+
+    def along(pairs):
+        return [(a * 4 + i, b * 4 + i) for a, b in pairs for i in range(4)]
+
+    def send_to(value, pairs):
+        return lax.ppermute(value, "tm", pairs)
+
+    arrived, kept = [], []
+    for i, (own, send) in enumerate(parts):
+        got = send_to(send, other_core)
+        away, stays = pl.pallas_call(
+            join_kernel, in_specs=[vmem] * 2, out_specs=[vmem] * 2, out_shape=[chunk()] * 2, compiler_params=limit(8)
+        )(own, got)
+        kept.append(stays)
+        arrived.append(send_to(away, other_y))
+
+    def added(*values):
+        return pl.pallas_call(
+            sum_kernel, in_specs=[vmem] * len(values), out_specs=vmem, out_shape=chunk(), compiler_params=limit(8)
+        )(*values)
+
+    scale = inverse_counts(words, owned_tile, slots, rows, inputs, samples // subs)
+    inwards = along([(0, 1), (3, 2)])
+    across = along([(1, 2), (2, 1)])
+    outwards = along([(1, 0), (2, 3)])
+    first = added(kept[0], arrived[0])
+    end0 = send_to(first, inwards)
+    second = added(kept[1], arrived[1])
+    end1 = send_to(second, inwards)
+    mid1 = send_to(added(second, end0), across)
+    third = added(kept[2], arrived[2])
+    end2 = send_to(third, inwards)
+    mid2 = send_to(added(third, end1), across)
+    back = send_to(added(first, mid1), outwards)
+
+    cells = slots // 2
+    message = [jax.ShapeDtypeStruct((2 * packs, rows, LANES), jnp.float32)] * (cells - 1)
+    message.append(jax.ShapeDtypeStruct((packs, rows, LANES), jnp.float32))
+    reduced, *outgoing = pl.pallas_call(
+        lambda *refs: mirror_kernel(*refs, channels=channels, rows=rows, slots=slots, span=span),
+        in_specs=[vmem] * 5,
+        out_specs=[vmem] * (cells + 1),
+        out_shape=[chunk()] + message,
+        scratch_shapes=[pltpu.VMEM((span - 1, 2 * packs, LANES, LANES), jnp.float32)],
+        compiler_params=limit(8),
+        name="mirror",
+    )(kept[-1], arrived[-1], end2, mid2, back)
+    incoming = [
+        send_to(value, [(d, (d + delta) % slots) for d in range(slots)])
+        for delta, value in enumerate(outgoing, 1)
+    ]
+    return pl.pallas_call(
+        lambda *refs: final_kernel(*refs, channels=channels, rows=rows, slots=slots, span=span),
+        in_specs=[smem] + [vmem] * (2 + cells),
+        out_specs=vmem,
+        out_shape=jax.ShapeDtypeStruct((rows, channels, 2, inputs), jnp.float32),
+        scratch_shapes=[
+            pltpu.VMEM((blocks + 2 * packs * (cells - 1) + packs, rows, LANES), jnp.float32),
+            pltpu.SMEM((slots,), jnp.int32),
+        ],
+        compiler_params=limit(12),
+        name="assemble",
+    )(owned_tile, reduced, scale, *incoming)
+
+
 def solution(mesh):
+    places = line_of_chips(mesh)
+
+    def shards(voltages, antenna_flags, owned_tile):
+        channels, _, inputs, samples = voltages.shape
+        slots = mesh.shape["tm"]
+        subs = antenna_flags.shape[0]
+        rows = inputs // slots
+        fits = (
+            places is not None
+            and rows * 4 == LANES
+            and inputs == places * LANES
+            and places == len(ORDER)
+            and channels % (LANES // rows) == 0
+            and slots & (slots - 1) == 0
+            and samples == subs * LANES
+        )
+        if fits:
+            return grid_shards(voltages, antenna_flags, owned_tile, places)
+        return plain_shards(voltages, antenna_flags, owned_tile)
+
     return jax.shard_map(
         shards,
         mesh=mesh,

time: 302 us -> 110 us (0.36)
  waiting for transfers between devices: 154 us -> 46.4 us
  local copies, waits for them, and re-layouts: 61.3 us -> 1.34 us
  starting transfers between devices: 0.01 us -> 39.5 us
  other arithmetic: 27.2 us -> 0.02 us
  blocking collectives: 23.1 us -> 0 us
  Pallas kernels: 0 us -> 21.5 us
  matrix products: 20.9 us -> 0 us
  between operations: 14.2 us -> 0.24 us
    reduce_scatter x1 -> x0, waiting for transfers between devices: 154 us -> none  [shards(): lax.psum_scatter(jnp.einsum('ckru,cju->rckj', picked, right_side, preferr...]
    ppermute x0 -> x26, waiting for transfers between devices: none -> 46.4 us  [the longest x22 39.8 us: send_to(): return lax.ppermute(value, 'tm', pairs)]
    ppermute x0 -> x26, starting transfers between devices: none -> 39.5 us  [the longest x22 32.6 us: send_to(): return lax.ppermute(value, 'tm', pairs)]
    gather x2 -> x0, local copies, waits for them, and re-layouts: 23.8 us -> none  [the longest x1 23.2 us: shards(): picked = jnp.take(left_side, row_index, axis=2)]
    all_gather x1 -> x0, blocking collectives: 23.1 us -> none  [shards(): every_word = lax.all_gather(antenna_flags, 'tm', axis=0, tiled=True)]
    pallas_call x0 -> x17, Pallas kernels: none -> 21.5 us  [the longest x3 10.1 us: grid_shards(): pl.pallas_call(lambda *refs: next_kernel(*refs, part=i, **size), in_specs...]
    dot_general x2 -> x0, matrix products: 20.9 us -> none  [the longest x1 20.3 us: shards(): jnp.einsum('ckru,cju->rckj', picked, right_side, preferred_element_type=j...]
    transpose x1 -> x0, local copies, waits for them, and re-layouts: 20.2 us -> none  [shards(): jnp.einsum('ckru,cju->rckj', picked, right_side, preferred_element_type=j...]
  transfers between devices with their start and end apart: 1 -> 26, of which waited for: 1 -> 12; matrix products, arithmetic and copies ran while one was open for 1% -> 0% of each run, Pallas kernels for 0% -> 11%
where the time goes in v1:
time: 110 us; the launch traced here: 109 us
  waiting for transfers between devices  46.4 us (42%)
  starting transfers between devices  39.5 us (36%)
  Pallas kernels  21.5 us (20%)
  local copies, waits for them, and re-layouts  1.34 us (1%)
    ppermute x22, waiting for transfers between devices, send_to(): return lax.ppermute(value, 'tm', pairs)  39.8 us
    ppermute x22, starting transfers between devices, send_to(): return lax.ppermute(value, 'tm', pairs)  32.6 us
    pallas_call x3, Pallas kernels, grid_shards(): pl.pallas_call(lambda *refs: next_kernel(*refs, part=i, **size), in_specs...  10.1 us
    ppermute x4, starting transfers between devices, inverse_counts(): lax.ppermute(words, 'tm', [(d, d ^ hop) for d in range(slots)])  6.95 us
    ppermute x4, waiting for transfers between devices, inverse_counts(): lax.ppermute(words, 'tm', [(d, d ^ hop) for d in range(slots)])  6.54 us
    pallas_call x1, Pallas kernels, grid_shards(): pl.pallas_call(lambda *refs: first_kernel(*refs, slots=slots, subs=subs,...  5.36 us
    pallas_call x1, Pallas kernels, grid_shards(): pl.pallas_call(lambda *refs: final_kernel(*refs, channels=channels, rows=...  4.06 us
  transfers between devices with their start and end apart: 26, of which 12 were waited for; matrix products, arithmetic and copies ran while one was open for 0% of the time, Pallas kernels for 11%

profile of v1, /device:TPU:0, one launch (start us, length us, event | category | flops | bytes accessed | tf_op | source)
XLA Modules:
  0.0 109.1 jit_solution(3381679806127355302)
XLA Ops:
  1.3 5.4 %mask_and_part.1 = (bf16[8,2,512,256]{3,2,1,0:T(8,128)(2,1)S(1)}, f32[2,34,32,128]{3,2,1,0:T(8,128)S(1)}, f32[2,34,32,128]{3,2,1,0:T(8,128)S(1)}, s32[32,8]{1,0:T(8,128)S(1)}) custom-call(s32[16]{0:T(128)S(1)} %copy-done, s32[2,8]{1,0:T(2,128)S(1)} %copy-done.2, bf16[8,2,512,256]{3,2,1,0:T(8,128)(2,1)} %refs_2_.1), custom_call_target="tpu_custom_call" | custom-call | flops 4294967296 | tf_op jit(solution)/shard_map/mask_and_part/pallas_call | solution.py:377
  7.3 3.4 %shard_map.42 = (f32[2,34,32,128]{3,2,1,0:T(8,128)S(1)}, f32[2,34,32,128]{3,2,1,0:T(8,128)S(1)}) custom-call(bf16[8,2,512,256]{3,2,1,0:T(8,128)(2,1)S(1)} %get-tuple-element.32.refs_0_), custom_call_target="tpu_custom_call" | custom-call | flops 4294967296 | tf_op jit(solution)/shard_map/pallas_call | solution.py:395
  10.7 3.4 %shard_map.39 = (f32[2,34,32,128]{3,2,1,0:T(8,128)S(1)}, f32[2,34,32,128]{3,2,1,0:T(8,128)S(1)}) custom-call(bf16[8,2,512,256]{3,2,1,0:T(8,128)(2,1)S(1)} %get-tuple-element.32.refs_0_), custom_call_target="tpu_custom_call" | custom-call | flops 4294967296 | tf_op jit(solution)/shard_map/pallas_call | solution.py:395
  14.8 2.6 %collective-permute-start.10 = (f32[34,32,128]{2,1,0:T(8,128)S(1)}, f32[34,32,128]{2,1,0:T(8,128)S(1)}, u32[]{:S(2)}, u32[]{:S(2)}) collective-permute-start(f32[34,32,128]{2,1,0:T(8,128)S(1)} %get-tuple-element.48), channel_id=1, source_target_pairs={{0,2},{1,3},{2,0},{3,1},{4,6},{5,7},{6,4},{7,5},{8,10},{9,11},{10,... | collective-permute-start | bytes 1671176 | tf_op jit(solution)/shard_map/ppermute | solution.py:413
  17.4 3.4 %shard_map.37 = (f32[2,34,32,128]{3,2,1,0:T(8,128)S(1)}, f32[2,34,32,128]{3,2,1,0:T(8,128)S(1)}) custom-call(bf16[8,2,512,256]{3,2,1,0:T(8,128)(2,1)S(1)} %get-tuple-element.32.refs_0_), custom_call_target="tpu_custom_call" | custom-call | flops 4294967296 | tf_op jit(solution)/shard_map/pallas_call | solution.py:395
  21.5 9.3 %collective-permute-done.10.refs_1_ = f32[34,32,128]{2,1,0:T(8,128)S(1)} collective-permute-done((f32[34,32,128]{2,1,0:T(8,128)S(1)}, f32[34,32,128]{2,1,0:T(8,128)S(1)}, u32[]{:S(2)}, u32[]{:S(2)}) %collective-permute-start.10) | collective-permute-done | bytes 557088 | tf_op jit(solution)/shard_map/ppermute | solution.py:413
  30.9 4.0 %collective-permute-start.11 = (f32[34,32,128]{2,1,0:T(8,128)S(1)}, f32[34,32,128]{2,1,0:T(8,128)S(1)}, u32[]{:S(2)}, u32[]{:S(2)}) collective-permute-start(f32[34,32,128]{2,1,0:T(8,128)S(1)} %shard_map.47.refs_0_), channel_id=1, source_target_pairs={{0,4},{1,5},{2,6},{3,7},{12,8},{13,9},{14,10},{15,11},{16,20},{17,... | collective-permute-start | bytes 1671176 | tf_op jit(solution)/shard_map/ppermute | solution.py:413
  36.7 6.1 %collective-permute-done.6.refs_1_ = f32[34,32,128]{2,1,0:T(8,128)S(1)} collective-permute-done((f32[34,32,128]{2,1,0:T(8,128)S(1)}, f32[34,32,128]{2,1,0:T(8,128)S(1)}, u32[]{:S(2)}, u32[]{:S(2)}) %collective-permute-start.6) | collective-permute-done | bytes 557088 | tf_op jit(solution)/shard_map/ppermute | solution.py:413
  42.9 4.0 %collective-permute-start.7 = (f32[34,32,128]{2,1,0:T(8,128)S(1)}, f32[34,32,128]{2,1,0:T(8,128)S(1)}, u32[]{:S(2)}, u32[]{:S(2)}) collective-permute-start(f32[34,32,128]{2,1,0:T(8,128)S(1)} %shard_map.44.refs_0_), channel_id=1, source_target_pairs={{0,4},{1,5},{2,6},{3,7},{12,8},{13,9},{14,10},{15,11},{16,20},{17,... | collective-permute-start | bytes 1671176 | tf_op jit(solution)/shard_map/ppermute | solution.py:413
  49.4 5.3 %collective-permute-done.3.refs_1_ = f32[34,32,128]{2,1,0:T(8,128)S(1)} collective-permute-done((f32[34,32,128]{2,1,0:T(8,128)S(1)}, f32[34,32,128]{2,1,0:T(8,128)S(1)}, u32[]{:S(2)}, u32[]{:S(2)}) %collective-permute-start.3) | collective-permute-done | bytes 557088 | tf_op jit(solution)/shard_map/ppermute | solution.py:413
  54.8 4.0 %collective-permute-start.4 = (f32[34,32,128]{2,1,0:T(8,128)S(1)}, f32[34,32,128]{2,1,0:T(8,128)S(1)}, u32[]{:S(2)}, u32[]{:S(2)}) collective-permute-start(f32[34,32,128]{2,1,0:T(8,128)S(1)} %shard_map.41.refs_0_), channel_id=1, source_target_pairs={{0,4},{1,5},{2,6},{3,7},{12,8},{13,9},{14,10},{15,11},{16,20},{17,... | collective-permute-start | bytes 1671176 | tf_op jit(solution)/shard_map/ppermute | solution.py:413
  61.0 5.5 %collective-permute-done.1.refs_1_ = f32[34,32,128]{2,1,0:T(8,128)S(1)} collective-permute-done((f32[34,32,128]{2,1,0:T(8,128)S(1)}, f32[34,32,128]{2,1,0:T(8,128)S(1)}, u32[]{:S(2)}, u32[]{:S(2)}) %collective-permute-start.1) | collective-permute-done | bytes 557088 | tf_op jit(solution)/shard_map/ppermute | solution.py:413
  66.5 3.5 %collective-permute-done.4.refs_2_ = f32[34,32,128]{2,1,0:T(8,128)S(1)} collective-permute-done((f32[34,32,128]{2,1,0:T(8,128)S(1)}, f32[34,32,128]{2,1,0:T(8,128)S(1)}, u32[]{:S(2)}, u32[]{:S(2)}) %collective-permute-start.4) | collective-permute-done | bytes 557088 | tf_op jit(solution)/shard_map/ppermute | solution.py:413
  69.9 6.2 %collective-permute-done.13.refs_4_ = f32[34,32,128]{2,1,0:T(8,128)S(1)} collective-permute-done((f32[34,32,128]{2,1,0:T(8,128)S(1)}, f32[34,32,128]{2,1,0:T(8,128)S(1)}, u32[]{:S(2)}, u32[]{:S(2)}) %collective-permute-start.13) | collective-permute-done | bytes 557088 | tf_op jit(solution)/shard_map/ppermute | solution.py:413
  78.2 1.7 %collective-permute-start.14 = (s32[32,8]{1,0:T(8,128)S(1)}, s32[32,8]{1,0:T(8,128)S(1)}, u32[]{:S(2)}, u32[]{:S(2)}) collective-permute-start(s32[32,8]{1,0:T(8,128)S(1)} %get-tuple-element.50), channel_id=1, source_target_pairs={{0,2},{1,3},{2,0},{3,1},{4,6},{5,7},{6,4},{7,5},{8,10},{9,11},{10,... | collective-permute-start | bytes 3080 | tf_op jit(solution)/shard_map/ppermute | solution.py:342
  79.9 2.0 %collective-permute-done.14 = s32[32,8]{1,0:T(8,128)S(1)} collective-permute-done((s32[32,8]{1,0:T(8,128)S(1)}, s32[32,8]{1,0:T(8,128)S(1)}, u32[]{:S(2)}, u32[]{:S(2)}) %collective-permute-start.14) | collective-permute-done | bytes 1056 | tf_op jit(solution)/shard_map/ppermute | solution.py:342
  83.1 2.2 %collective-permute-start.16 = (s32[32,8]{1,0:T(8,128)S(1)}, s32[32,8]{1,0:T(8,128)S(1)}, u32[]{:S(2)}, u32[]{:S(2)}) collective-permute-start(s32[32,8]{1,0:T(8,128)S(1)} %add.13), channel_id=1, source_target_pairs={{0,4},{1,5},{2,6},{3,7},{4,0},{5,1},{6,2},{7,3},{8,12},{9,13},{10,... | collective-permute-start | bytes 3080 | tf_op jit(solution)/shard_map/ppermute | solution.py:342
  87.0 2.6 %collective-permute-start.17 = (s32[32,8]{1,0:T(8,128)S(1)}, s32[32,8]{1,0:T(8,128)S(1)}, u32[]{:S(2)}, u32[]{:S(2)}) collective-permute-start(s32[32,8]{1,0:T(8,128)S(1)} %add.14), channel_id=1, source_target_pairs={{0,8},{1,9},{2,10},{3,11},{4,12},{5,13},{6,14},{7,15},{8,0},{9,1},... | collective-permute-start | bytes 3080 | tf_op jit(solution)/shard_map/ppermute | solution.py:342
  89.7 2.0 %collective-permute-done.17 = s32[32,8]{1,0:T(8,128)S(1)} collective-permute-done((s32[32,8]{1,0:T(8,128)S(1)}, s32[32,8]{1,0:T(8,128)S(1)}, u32[]{:S(2)}, u32[]{:S(2)}) %collective-permute-start.17) | collective-permute-done | bytes 1056 | tf_op jit(solution)/shard_map/ppermute | solution.py:342
  91.7 2.0 %collective-permute-start.21 = (f32[4,32,128]{2,1,0:T(8,128)S(1)}, f32[4,32,128]{2,1,0:T(8,128)S(1)}, u32[]{:S(2)}, u32[]{:S(2)}) collective-permute-start(f32[4,32,128]{2,1,0:T(8,128)S(1)} %get-tuple-element.54), channel_id=1, source_target_pairs={{0,4},{1,5},{2,6},{3,7},{4,8},{5,9},{6,10},{7,11},{8,12},{9,13},{1... | collective-permute-start | bytes 196616 | tf_op jit(solution)/shard_map/ppermute | solution.py:413
  93.7 1.8 %collective-permute-start.23 = (f32[4,32,128]{2,1,0:T(8,128)S(1)}, f32[4,32,128]{2,1,0:T(8,128)S(1)}, u32[]{:S(2)}, u32[]{:S(2)}) collective-permute-start(f32[4,32,128]{2,1,0:T(8,128)S(1)} %get-tuple-element.56), channel_id=1, source_target_pairs={{0,6},{1,7},{2,8},{3,9},{4,10},{5,11},{6,12},{7,13},{8,14},{9,15},... | collective-permute-start | bytes 196616 | tf_op jit(solution)/shard_map/ppermute | solution.py:413
  95.5 4.7 %collective-permute-start.24 = (f32[4,32,128]{2,1,0:T(8,128)S(1)}, f32[4,32,128]{2,1,0:T(8,128)S(1)}, u32[]{:S(2)}, u32[]{:S(2)}) collective-permute-start(f32[4,32,128]{2,1,0:T(8,128)S(1)} %get-tuple-element.57), channel_id=1, source_target_pairs={{0,7},{1,8},{2,9},{3,10},{4,11},{5,12},{6,13},{7,14},{8,15},{9,0},... | collective-permute-start | bytes 196616 | tf_op jit(solution)/shard_map/ppermute | solution.py:413
  101.2 3.4 %collective-permute-done.22.refs_7_ = f32[4,32,128]{2,1,0:T(8,128)S(1)} collective-permute-done((f32[4,32,128]{2,1,0:T(8,128)S(1)}, f32[4,32,128]{2,1,0:T(8,128)S(1)}, u32[]{:S(2)}, u32[]{:S(2)}) %collective-permute-start.22) | collective-permute-done | bytes 65568 | tf_op jit(solution)/shard_map/ppermute | solution.py:413
  105.0 4.1 %assemble.1 = f32[32,8,2,512]{3,2,1,0:T(2,128)} custom-call(s32[16]{0:T(128)S(1)} %copy-done.1, f32[34,32,128]{2,1,0:T(8,128)S(1)} %get-tuple-element.49.refs_1_, f32[32,512]{1,0:T(8,128)S(1)} %scale.1.refs_2_, f32[4,32,128]{2,1,0:T(8,128)S(1)} %collective-permute-done.18.refs_3_, f32[4,32,128]{2,1,0:T(8,128)S(1)} %collective-permute-done.19.refs_4_, ...), custom_call_target="tpu_custom_call" | custom-call | tf_op jit(solution)/shard_map/assemble/pallas_call | solution.py:459
  (55 shorter events, 16.2 us)
Async XLA Ops:
  6.7 7.9 %collective-permute-start.9 = (f32[2,34,32,128]{3,2,1,0:T(8,128)S(1)}, f32[2,34,32,128]{3,2,1,0:T(8,128)S(1)}, u32[]{:S(2)}, u32[]{:S(2)}) collective-permute-start(f32[2,34,32,128]{3,2,1,0:T(8,128)S(1)} %get-tuple-element.46), channel_id=1, source_target_pairs={{0,1},{1,0},{2,3},{3,2},{4,5},{5,4},{6,7},{7,6},{8,9},{9,8},{10,11... | collective-permute-start | bytes 3342344 | tf_op jit(solution)/shard_map/ppermute | solution.py:413
  10.6 10.4 %collective-permute-start.5 = (f32[2,34,32,128]{3,2,1,0:T(8,128)S(1)}, f32[2,34,32,128]{3,2,1,0:T(8,128)S(1)}, u32[]{:S(2)}, u32[]{:S(2)}) collective-permute-start(f32[2,34,32,128]{3,2,1,0:T(8,128)S(1)} %get-tuple-element.42), channel_id=1, source_target_pairs={{0,1},{1,0},{2,3},{3,2},{4,5},{5,4},{6,7},{7,6},{8,9},{9,8},{10,11... | collective-permute-start | bytes 3342344 | tf_op jit(solution)/shard_map/ppermute | solution.py:413
  14.1 20.8 %collective-permute-start.2 = (f32[2,34,32,128]{3,2,1,0:T(8,128)S(1)}, f32[2,34,32,128]{3,2,1,0:T(8,128)S(1)}, u32[]{:S(2)}, u32[]{:S(2)}) collective-permute-start(f32[2,34,32,128]{3,2,1,0:T(8,128)S(1)} %get-tuple-element.38), channel_id=1, source_target_pairs={{0,1},{1,0},{2,3},{3,2},{4,5},{5,4},{6,7},{7,6},{8,9},{9,8},{10,11... | collective-permute-start | bytes 3342344 | tf_op jit(solution)/shard_map/ppermute | solution.py:413
  14.8 16.1 %collective-permute-start.10 = (f32[34,32,128]{2,1,0:T(8,128)S(1)}, f32[34,32,128]{2,1,0:T(8,128)S(1)}, u32[]{:S(2)}, u32[]{:S(2)}) collective-permute-start(f32[34,32,128]{2,1,0:T(8,128)S(1)} %get-tuple-element.48), channel_id=1, source_target_pairs={{0,2},{1,3},{2,0},{3,1},{4,6},{5,7},{6,4},{7,5},{8,10},{9,11},{10,... | collective-permute-start | bytes 1671176 | tf_op jit(solution)/shard_map/ppermute | solution.py:413
  20.7 26.9 %collective-permute-start = (f32[2,34,32,128]{3,2,1,0:T(8,128)S(1)}, f32[2,34,32,128]{3,2,1,0:T(8,128)S(1)}, u32[]{:S(2)}, u32[]{:S(2)}) collective-permute-start(f32[2,34,32,128]{3,2,1,0:T(8,128)S(1)} %get-tuple-element.34), channel_id=1, source_target_pairs={{0,1},{1,0},{2,3},{3,2},{4,5},{5,4},{6,7},{7,6},{8,9},{9,8},{10,11... | collective-permute-start | bytes 3342344 | tf_op jit(solution)/shard_map/ppermute | solution.py:413
  21.1 21.7 %collective-permute-start.6 = (f32[34,32,128]{2,1,0:T(8,128)S(1)}, f32[34,32,128]{2,1,0:T(8,128)S(1)}, u32[]{:S(2)}, u32[]{:S(2)}) collective-permute-start(f32[34,32,128]{2,1,0:T(8,128)S(1)} %get-tuple-element.44), channel_id=1, source_target_pairs={{0,2},{1,3},{2,0},{3,1},{4,6},{5,7},{6,4},{7,5},{8,10},{9,11},{10,... | collective-permute-start | bytes 1671176 | tf_op jit(solution)/shard_map/ppermute | solution.py:413
  30.9 16.0 %collective-permute-start.11 = (f32[34,32,128]{2,1,0:T(8,128)S(1)}, f32[34,32,128]{2,1,0:T(8,128)S(1)}, u32[]{:S(2)}, u32[]{:S(2)}) collective-permute-start(f32[34,32,128]{2,1,0:T(8,128)S(1)} %shard_map.47.refs_0_), channel_id=1, source_target_pairs={{0,4},{1,5},{2,6},{3,7},{12,8},{13,9},{14,10},{15,11},{16,20},{17,... | collective-permute-start | bytes 1671176 | tf_op jit(solution)/shard_map/ppermute | solution.py:413
  35.1 19.7 %collective-permute-start.3 = (f32[34,32,128]{2,1,0:T(8,128)S(1)}, f32[34,32,128]{2,1,0:T(8,128)S(1)}, u32[]{:S(2)}, u32[]{:S(2)}) collective-permute-start(f32[34,32,128]{2,1,0:T(8,128)S(1)} %get-tuple-element.40), channel_id=1, source_target_pairs={{0,2},{1,3},{2,0},{3,1},{4,6},{5,7},{6,4},{7,5},{8,10},{9,11},{10,... | collective-permute-start | bytes 1671176 | tf_op jit(solution)/shard_map/ppermute | solution.py:413
  42.9 16.0 %collective-permute-start.7 = (f32[34,32,128]{2,1,0:T(8,128)S(1)}, f32[34,32,128]{2,1,0:T(8,128)S(1)}, u32[]{:S(2)}, u32[]{:S(2)}) collective-permute-start(f32[34,32,128]{2,1,0:T(8,128)S(1)} %shard_map.44.refs_0_), channel_id=1, source_target_pairs={{0,4},{1,5},{2,6},{3,7},{12,8},{13,9},{14,10},{15,11},{16,20},{17,... | collective-permute-start | bytes 1671176 | tf_op jit(solution)/shard_map/ppermute | solution.py:413
  47.0 12.6 %collective-permute-start.12 = (f32[34,32,128]{2,1,0:T(8,128)S(1)}, f32[34,32,128]{2,1,0:T(8,128)S(1)}, u32[]{:S(2)}, u32[]{:S(2)}) collective-permute-start(f32[34,32,128]{2,1,0:T(8,128)S(1)} %shard_map.48), channel_id=1, source_target_pairs={{4,8},{5,9},{6,10},{7,11},{8,4},{9,5},{10,6},{11,7},{20,24},{21,25... | collective-permute-start | bytes 1671176 | tf_op jit(solution)/shard_map/ppermute | solution.py:413
  47.8 18.7 %collective-permute-start.1 = (f32[34,32,128]{2,1,0:T(8,128)S(1)}, f32[34,32,128]{2,1,0:T(8,128)S(1)}, u32[]{:S(2)}, u32[]{:S(2)}) collective-permute-start(f32[34,32,128]{2,1,0:T(8,128)S(1)} %get-tuple-element.36), channel_id=1, source_target_pairs={{0,2},{1,3},{2,0},{3,1},{4,6},{5,7},{6,4},{7,5},{8,10},{9,11},{10,... | collective-permute-start | bytes 1671176 | tf_op jit(solution)/shard_map/ppermute | solution.py:413
  54.8 15.1 %collective-permute-start.4 = (f32[34,32,128]{2,1,0:T(8,128)S(1)}, f32[34,32,128]{2,1,0:T(8,128)S(1)}, u32[]{:S(2)}, u32[]{:S(2)}) collective-permute-start(f32[34,32,128]{2,1,0:T(8,128)S(1)} %shard_map.41.refs_0_), channel_id=1, source_target_pairs={{0,4},{1,5},{2,6},{3,7},{12,8},{13,9},{14,10},{15,11},{16,20},{17,... | collective-permute-start | bytes 1671176 | tf_op jit(solution)/shard_map/ppermute | solution.py:413
  58.9 11.0 %collective-permute-start.8 = (f32[34,32,128]{2,1,0:T(8,128)S(1)}, f32[34,32,128]{2,1,0:T(8,128)S(1)}, u32[]{:S(2)}, u32[]{:S(2)}) collective-permute-start(f32[34,32,128]{2,1,0:T(8,128)S(1)} %shard_map.45), channel_id=1, source_target_pairs={{4,8},{5,9},{6,10},{7,11},{8,4},{9,5},{10,6},{11,7},{20,24},{21,25... | collective-permute-start | bytes 1671176 | tf_op jit(solution)/shard_map/ppermute | solution.py:413
  59.7 16.4 %collective-permute-start.13 = (f32[34,32,128]{2,1,0:T(8,128)S(1)}, f32[34,32,128]{2,1,0:T(8,128)S(1)}, u32[]{:S(2)}, u32[]{:S(2)}) collective-permute-start(f32[34,32,128]{2,1,0:T(8,128)S(1)} %shard_map.49), channel_id=1, source_target_pairs={{4,0},{5,1},{6,2},{7,3},{8,12},{9,13},{10,14},{11,15},{20,16},{21,... | collective-permute-start | bytes 1671176 | tf_op jit(solution)/shard_map/ppermute | solution.py:413
  76.4 17.3 %collective-permute-start.18 = (f32[4,32,128]{2,1,0:T(8,128)S(1)}, f32[4,32,128]{2,1,0:T(8,128)S(1)}, u32[]{:S(2)}, u32[]{:S(2)}) collective-permute-start(f32[4,32,128]{2,1,0:T(8,128)S(1)} %get-tuple-element.51), channel_id=1, source_target_pairs={{0,1},{1,2},{2,3},{3,4},{4,5},{5,6},{6,7},{7,8},{8,9},{9,10},{10,1... | collective-permute-start | bytes 196616 | tf_op jit(solution)/shard_map/ppermute | solution.py:413
  76.5 19.0 %collective-permute-start.19 = (f32[4,32,128]{2,1,0:T(8,128)S(1)}, f32[4,32,128]{2,1,0:T(8,128)S(1)}, u32[]{:S(2)}, u32[]{:S(2)}) collective-permute-start(f32[4,32,128]{2,1,0:T(8,128)S(1)} %get-tuple-element.52), channel_id=1, source_target_pairs={{0,2},{1,3},{2,4},{3,5},{4,6},{5,7},{6,8},{7,9},{8,10},{9,11},{10,... | collective-permute-start | bytes 196616 | tf_op jit(solution)/shard_map/ppermute | solution.py:413
  78.1 15.6 %collective-permute-start.25 = (f32[2,32,128]{2,1,0:T(8,128)S(1)}, f32[2,32,128]{2,1,0:T(8,128)S(1)}, u32[]{:S(2)}, u32[]{:S(2)}) collective-permute-start(f32[2,32,128]{2,1,0:T(8,128)S(1)} %get-tuple-element.58), channel_id=1, source_target_pairs={{0,8},{1,9},{2,10},{3,11},{4,12},{5,13},{6,14},{7,15},{8,0},{9,1},... | collective-permute-start | bytes 98312 | tf_op jit(solution)/shard_map/ppermute | solution.py:413
  83.1 3.9 %collective-permute-start.16 = (s32[32,8]{1,0:T(8,128)S(1)}, s32[32,8]{1,0:T(8,128)S(1)}, u32[]{:S(2)}, u32[]{:S(2)}) collective-permute-start(s32[32,8]{1,0:T(8,128)S(1)} %add.13), channel_id=1, source_target_pairs={{0,4},{1,5},{2,6},{3,7},{4,0},{5,1},{6,2},{7,3},{8,12},{9,13},{10,... | collective-permute-start | bytes 3080 | tf_op jit(solution)/shard_map/ppermute | solution.py:342
  87.0 4.6 %collective-permute-start.17 = (s32[32,8]{1,0:T(8,128)S(1)}, s32[32,8]{1,0:T(8,128)S(1)}, u32[]{:S(2)}, u32[]{:S(2)}) collective-permute-start(s32[32,8]{1,0:T(8,128)S(1)} %add.14), channel_id=1, source_target_pairs={{0,8},{1,9},{2,10},{3,11},{4,12},{5,13},{6,14},{7,15},{8,0},{9,1},... | collective-permute-start | bytes 3080 | tf_op jit(solution)/shard_map/ppermute | solution.py:342
  89.7 11.5 %collective-permute-start.20 = (f32[4,32,128]{2,1,0:T(8,128)S(1)}, f32[4,32,128]{2,1,0:T(8,128)S(1)}, u32[]{:S(2)}, u32[]{:S(2)}) collective-permute-start(f32[4,32,128]{2,1,0:T(8,128)S(1)} %get-tuple-element.53), channel_id=1, source_target_pairs={{0,3},{1,4},{2,5},{3,6},{4,7},{5,8},{6,9},{7,10},{8,11},{9,12},{10... | collective-permute-start | bytes 196616 | tf_op jit(solution)/shard_map/ppermute | solution.py:413
  91.7 9.5 %collective-permute-start.21 = (f32[4,32,128]{2,1,0:T(8,128)S(1)}, f32[4,32,128]{2,1,0:T(8,128)S(1)}, u32[]{:S(2)}, u32[]{:S(2)}) collective-permute-start(f32[4,32,128]{2,1,0:T(8,128)S(1)} %get-tuple-element.54), channel_id=1, source_target_pairs={{0,4},{1,5},{2,6},{3,7},{4,8},{5,9},{6,10},{7,11},{8,12},{9,13},{1... | collective-permute-start | bytes 196616 | tf_op jit(solution)/shard_map/ppermute | solution.py:413
  93.7 10.9 %collective-permute-start.22 = (f32[4,32,128]{2,1,0:T(8,128)S(1)}, f32[4,32,128]{2,1,0:T(8,128)S(1)}, u32[]{:S(2)}, u32[]{:S(2)}) collective-permute-start(f32[4,32,128]{2,1,0:T(8,128)S(1)} %get-tuple-element.55), channel_id=1, source_target_pairs={{0,5},{1,6},{2,7},{3,8},{4,9},{5,10},{6,11},{7,12},{8,13},{9,14},{... | collective-permute-start | bytes 196616 | tf_op jit(solution)/shard_map/ppermute | solution.py:413
  93.7 11.3 %collective-permute-start.23 = (f32[4,32,128]{2,1,0:T(8,128)S(1)}, f32[4,32,128]{2,1,0:T(8,128)S(1)}, u32[]{:S(2)}, u32[]{:S(2)}) collective-permute-start(f32[4,32,128]{2,1,0:T(8,128)S(1)} %get-tuple-element.56), channel_id=1, source_target_pairs={{0,6},{1,7},{2,8},{3,9},{4,10},{5,11},{6,12},{7,13},{8,14},{9,15},... | collective-permute-start | bytes 196616 | tf_op jit(solution)/shard_map/ppermute | solution.py:413
  95.5 9.5 %collective-permute-start.24 = (f32[4,32,128]{2,1,0:T(8,128)S(1)}, f32[4,32,128]{2,1,0:T(8,128)S(1)}, u32[]{:S(2)}, u32[]{:S(2)}) collective-permute-start(f32[4,32,128]{2,1,0:T(8,128)S(1)} %get-tuple-element.57), channel_id=1, source_target_pairs={{0,7},{1,8},{2,9},{3,10},{4,11},{5,12},{6,13},{7,14},{8,15},{9,0},... | collective-permute-start | bytes 196616 | tf_op jit(solution)/shard_map/ppermute | solution.py:413
  (5 other events, 30.3 us)
